TPU v7x, 128 devices: a whole 4x4x4 slice. The times are simulated.
128 devices in a mesh: part: 1, data: 2 (over core), time: 64 (over z, y, x).
Axes of the slice: x: 4, y: 4, z: 4, core: 2. Of those that a mesh axis runs over, the one named last changes fastest.
Arguments:
- x_init: float32 [4, 4096, 16], P(('part', 'data'))
- w_in: bfloat16 [16, 1152], replicated
- w_out: bfloat16 [1152, 16], replicated
- mod_scale: bfloat16 [128, 1152], P('time')
- mod_shift: bfloat16 [128, 1152], P('time')
- step_size: float32 [128], P('time')
Outputs:
- output: float32 [128, 4, 4096, 16], P('time', ('part', 'data'))
All inputs are finite; a program needn't handle non-finite values.
Results may differ from a plain program's by a relative error of at most 0.001.
Values are sent between devices in bfloat16 or wider.
A program may use at most 1 GiB of HBM per device.

v0:
```python
import jax
import jax.numpy as jnp
from jax import lax
from jax.sharding import PartitionSpec as P

SWEEPS = 4


def drift_of(latents, w_in, w_out, scale_one, shift_val, step_size):
    pre = jnp.einsum("kbnc,ch->kbnh", latents.astype(jnp.bfloat16), w_in, preferred_element_type=jnp.float32)
    act = jax.nn.gelu(pre * scale_one[:, None, None, :] + shift_val[:, None, None, :], approximate=True)
    out = jnp.einsum("kbnh,hc->kbnc", act.astype(jnp.bfloat16), w_out, preferred_element_type=jnp.float32)
    return out * step_size[:, None, None, None]


def solution(mesh):
    time_size = mesh.shape["time"]
    hop_shifts = [1 << level for level in range(32) if (1 << level) < time_size]

    def local_run(x_init, w_in, w_out, mod_scale, mod_shift, step_size):
        scale_one = 1.0 + mod_scale.astype(jnp.float32)
        shift_val = mod_shift.astype(jnp.float32)
        latents = jnp.broadcast_to(x_init[None], (step_size.shape[0],) + x_init.shape)
        for sweep_index in range(SWEEPS):
            drift = drift_of(latents, w_in, w_out, scale_one, shift_val, step_size)
            running = jnp.cumsum(drift, axis=0)
            dev_total = running[-1]
            inclusive = dev_total
            for hop_shift in hop_shifts:
                pairs = [(source, source + hop_shift) for source in range(time_size - hop_shift)]
                inclusive = inclusive + lax.ppermute(inclusive, "time", pairs)
            offset = inclusive - dev_total
            latents = x_init[None] + offset[None] + (running - drift)
        return latents

    return jax.shard_map(
        local_run,
        mesh=mesh,
        in_specs=(P(("part", "data"), None, None), P(None, None), P(None, None), P("time", None), P("time", None), P("time")),
        out_specs=P("time", ("part", "data"), None, None),
        check_vma=False,
    )
```

profile of v0, /device:TPU:0, one launch (start us, length us, event | category | flops | bytes accessed | tf_op | source)
XLA Modules:
  0.0 513.7 jit_solution(10851073762134362414)
XLA Ops:
  2.5 32.8 %fusion.36 = f32[2,2,4096,16]{2,3,1,0:T(8,128)S(1)} fusion(f32[2,1152]{1,0:T(2,128)S(1)} %convert_element_type.33, f32[2,1152]{1,0:T(2,128)S(1)} %convert_add_fusion, f32[2]{0:T(128)} %param.11, bf16[2,4096,16]{1,2,0:T(8,128)(2,1)S(1)} %convert_element_type.31, bf16[1152,16]{0,1:T(8,128)(2,1)S(1)} %copy-done, bf16[16,1152]{1,0:T(8,128)(2,1)} %param.7), kind=kOutput, calls=%fused_computation.40 | convolution fusion | flops 1415839744 | bytes 1402888 | tf_op jit(solution)/shard_map/kbnh,hc->kbnc/dot_general | solution.py:12
  42.2 11.1 %collective-permute-done = f32[2,4096,16]{1,2,0:T(8,128)S(1)} collective-permute-done((f32[2,4096,16]{1,2,0:T(8,128)S(1)}, f32[2,4096,16]{1,2,0:T(8,128)S(1)}, u32[]{:S(2)}, u32[]{:S(2)}) %collective-permute-start) | collective-permute-done | bytes 524320 | tf_op jit(solution)/shard_map/ppermute | solution.py:31
  59.3 10.5 %collective-permute-done.1 = f32[2,4096,16]{1,2,0:T(8,128)S(1)} collective-permute-done((f32[2,4096,16]{1,2,0:T(8,128)S(1)}, f32[2,4096,16]{1,2,0:T(8,128)S(1)}, u32[]{:S(2)}, u32[]{:S(2)}) %collective-permute-start.1) | collective-permute-done | bytes 524320 | tf_op jit(solution)/shard_map/ppermute | solution.py:31
  69.9 7.8 %collective-permute-start.2 = (f32[2,4096,16]{1,2,0:T(8,128)S(1)}, f32[2,4096,16]{1,2,0:T(8,128)S(1)}, u32[]{:S(2)}, u32[]{:S(2)}) collective-permute-start(f32[2,4096,16]{1,2,0:T(8,128)S(1)} %add.183), channel_id=1, source_target_pairs={{0,4},{1,5},{2,6},{3,7},{4,8},{5,9},{6,10},{7,11},{8,12},{9,13},{1... | collective-permute-start | bytes 1572872 | tf_op jit(solution)/shard_map/ppermute | solution.py:31
  77.7 8.6 %collective-permute-done.2 = f32[2,4096,16]{1,2,0:T(8,128)S(1)} collective-permute-done((f32[2,4096,16]{1,2,0:T(8,128)S(1)}, f32[2,4096,16]{1,2,0:T(8,128)S(1)}, u32[]{:S(2)}, u32[]{:S(2)}) %collective-permute-start.2) | collective-permute-done | bytes 524320 | tf_op jit(solution)/shard_map/ppermute | solution.py:31
  92.4 8.1 %collective-permute-done.3 = f32[2,4096,16]{1,2,0:T(8,128)S(1)} collective-permute-done((f32[2,4096,16]{1,2,0:T(8,128)S(1)}, f32[2,4096,16]{1,2,0:T(8,128)S(1)}, u32[]{:S(2)}, u32[]{:S(2)}) %collective-permute-start.3) | collective-permute-done | bytes 524320 | tf_op jit(solution)/shard_map/ppermute | solution.py:31
  100.6 11.6 %collective-permute-start.4 = (f32[2,4096,16]{1,2,0:T(8,128)S(1)}, f32[2,4096,16]{1,2,0:T(8,128)S(1)}, u32[]{:S(2)}, u32[]{:S(2)}) collective-permute-start(f32[2,4096,16]{1,2,0:T(8,128)S(1)} %add.185), channel_id=1, source_target_pairs={{0,16},{1,17},{2,18},{3,19},{4,20},{5,21},{6,22},{7,23},{8,24},{9,... | collective-permute-start | bytes 1572872 | tf_op jit(solution)/shard_map/ppermute | solution.py:31
  118.9 12.2 %collective-permute-start.5 = (f32[2,4096,16]{1,2,0:T(8,128)S(1)}, f32[2,4096,16]{1,2,0:T(8,128)S(1)}, u32[]{:S(2)}, u32[]{:S(2)}) collective-permute-start(f32[2,4096,16]{1,2,0:T(8,128)S(1)} %add.186), channel_id=1, source_target_pairs={{0,32},{1,33},{2,34},{3,35},{4,36},{5,37},{6,38},{7,39},{8,40},{9,... | collective-permute-start | bytes 1572872 | tf_op jit(solution)/shard_map/ppermute | solution.py:31
  137.8 33.9 %fusion.37 = f32[2,2,4096,16]{2,3,1,0:T(8,128)S(1)} fusion(f32[2,1152]{1,0:T(2,128)S(1)} %convert_element_type.33, f32[2,1152]{1,0:T(2,128)S(1)} %convert_add_fusion, f32[2,2,4096,16]{2,3,1,0:T(8,128)S(1)} %fusion.80, f32[2,2,4096,16]{2,3,1,0:T(8,128)} %copy-done.2, f32[2,4096,16]{1,2,0:T(8,128)S(1)} %subtract_add_fusion.4, f32[2]{0:T(128)S(1)} %copy-done.4, ...), kind=kOutput, calls=%fused_computation.41 | convolution fusion | flops 1416626176 | bytes 3762184 | tf_op jit(solution)/shard_map/kbnh,hc->kbnc/dot_general | solution.py:12
  176.2 7.6 %collective-permute-done.6 = f32[2,4096,16]{1,2,0:T(8,128)S(1)} collective-permute-done((f32[2,4096,16]{1,2,0:T(8,128)S(1)}, f32[2,4096,16]{1,2,0:T(8,128)S(1)}, u32[]{:S(2)}, u32[]{:S(2)}) %collective-permute-start.6) | collective-permute-done | bytes 524320 | tf_op jit(solution)/shard_map/ppermute | solution.py:31
  200.4 10.9 %collective-permute-done.8 = f32[2,4096,16]{1,2,0:T(8,128)S(1)} collective-permute-done((f32[2,4096,16]{1,2,0:T(8,128)S(1)}, f32[2,4096,16]{1,2,0:T(8,128)S(1)}, u32[]{:S(2)}, u32[]{:S(2)}) %collective-permute-start.8) | collective-permute-done | bytes 524320 | tf_op jit(solution)/shard_map/ppermute | solution.py:31
  211.4 11.0 %collective-permute-start.9 = (f32[2,4096,16]{1,2,0:T(8,128)S(1)}, f32[2,4096,16]{1,2,0:T(8,128)S(1)}, u32[]{:S(2)}, u32[]{:S(2)}) collective-permute-start(f32[2,4096,16]{1,2,0:T(8,128)S(1)} %add.196), channel_id=1, source_target_pairs={{0,8},{1,9},{2,10},{3,11},{4,12},{5,13},{6,14},{7,15},{8,16},{9,17... | collective-permute-start | bytes 1572872 | tf_op jit(solution)/shard_map/ppermute | solution.py:31
  229.1 14.9 %collective-permute-start.10 = (f32[2,4096,16]{1,2,0:T(8,128)S(1)}, f32[2,4096,16]{1,2,0:T(8,128)S(1)}, u32[]{:S(2)}, u32[]{:S(2)}) collective-permute-start(f32[2,4096,16]{1,2,0:T(8,128)S(1)} %add.197), channel_id=1, source_target_pairs={{0,16},{1,17},{2,18},{3,19},{4,20},{5,21},{6,22},{7,23},{8,24},{9,... | collective-permute-start | bytes 1572872 | tf_op jit(solution)/shard_map/ppermute | solution.py:31
  244.1 7.6 %collective-permute-done.10 = f32[2,4096,16]{1,2,0:T(8,128)S(1)} collective-permute-done((f32[2,4096,16]{1,2,0:T(8,128)S(1)}, f32[2,4096,16]{1,2,0:T(8,128)S(1)}, u32[]{:S(2)}, u32[]{:S(2)}) %collective-permute-start.10) | collective-permute-done | bytes 524320 | tf_op jit(solution)/shard_map/ppermute | solution.py:31
  265.4 33.6 %fusion.38 = f32[2,2,4096,16]{2,3,1,0:T(8,128)} fusion(f32[2,1152]{1,0:T(2,128)S(1)} %convert_element_type.33, f32[2,1152]{1,0:T(2,128)S(1)} %convert_add_fusion, f32[2,2,4096,16]{2,3,1,0:T(8,128)S(1)} %fusion.81, f32[2,2,4096,16]{2,3,1,0:T(8,128)S(1)} %fusion.37, f32[2,4096,16]{1,2,0:T(8,128)S(1)} %subtract_add_fusion.3, f32[2]{0:T(128)S(1)} %copy-done.4, ...), kind=kOutput, calls=%fused_computation.42 | convolution fusion | flops 1416626176 | bytes 3762184 | tf_op jit(solution)/shard_map/kbnh,hc->kbnc/dot_general | solution.py:12
  318.9 11.3 %collective-permute-start.14 = (f32[2,4096,16]{1,2,0:T(8,128)S(1)}, f32[2,4096,16]{1,2,0:T(8,128)S(1)}, u32[]{:S(2)}, u32[]{:S(2)}) collective-permute-start(f32[2,4096,16]{1,2,0:T(8,128)S(1)} %add.207), channel_id=1, source_target_pairs={{0,4},{1,5},{2,6},{3,7},{4,8},{5,9},{6,10},{7,11},{8,12},{9,13},{1... | collective-permute-start | bytes 1572872 | tf_op jit(solution)/shard_map/ppermute | solution.py:31
  350.2 12.4 %collective-permute-start.16 = (f32[2,4096,16]{1,2,0:T(8,128)S(1)}, f32[2,4096,16]{1,2,0:T(8,128)S(1)}, u32[]{:S(2)}, u32[]{:S(2)}) collective-permute-start(f32[2,4096,16]{1,2,0:T(8,128)S(1)} %add.209), channel_id=1, source_target_pairs={{0,16},{1,17},{2,18},{3,19},{4,20},{5,21},{6,22},{7,23},{8,24},{9,... | collective-permute-start | bytes 1572872 | tf_op jit(solution)/shard_map/ppermute | solution.py:31
  362.6 9.5 %collective-permute-done.16 = f32[2,4096,16]{1,2,0:T(8,128)S(1)} collective-permute-done((f32[2,4096,16]{1,2,0:T(8,128)S(1)}, f32[2,4096,16]{1,2,0:T(8,128)S(1)}, u32[]{:S(2)}, u32[]{:S(2)}) %collective-permute-start.16) | collective-permute-done | bytes 524320 | tf_op jit(solution)/shard_map/ppermute | solution.py:31
  372.1 8.6 %collective-permute-start.17 = (f32[2,4096,16]{1,2,0:T(8,128)S(1)}, f32[2,4096,16]{1,2,0:T(8,128)S(1)}, u32[]{:S(2)}, u32[]{:S(2)}) collective-permute-start(f32[2,4096,16]{1,2,0:T(8,128)S(1)} %add.210), channel_id=1, source_target_pairs={{0,32},{1,33},{2,34},{3,35},{4,36},{5,37},{6,38},{7,39},{8,40},{9,... | collective-permute-start | bytes 1572872 | tf_op jit(solution)/shard_map/ppermute | solution.py:31
  387.2 33.9 %fusion.39 = f32[2,2,4096,16]{2,3,1,0:T(8,128)S(1)} fusion(f32[2,1152]{1,0:T(2,128)S(1)} %convert_element_type.33, f32[2,1152]{1,0:T(2,128)S(1)} %convert_add_fusion, f32[2,2,4096,16]{2,3,1,0:T(8,128)S(1)} %fusion.82, f32[2,2,4096,16]{2,3,1,0:T(8,128)} %fusion.38, f32[2,4096,16]{1,2,0:T(8,128)S(1)} %subtract_add_fusion.2, f32[2]{0:T(128)S(1)} %copy-done.4, ...), kind=kOutput, calls=%fused_computation.43 | convolution fusion | flops 1416626176 | bytes 3762184 | tf_op jit(solution)/shard_map/kbnh,hc->kbnc/dot_general | solution.py:12
  440.4 13.4 %collective-permute-start.20 = (f32[2,4096,16]{1,2,0:T(8,128)S(1)}, f32[2,4096,16]{1,2,0:T(8,128)S(1)}, u32[]{:S(2)}, u32[]{:S(2)}) collective-permute-start(f32[2,4096,16]{1,2,0:T(8,128)S(1)} %add.219), channel_id=1, source_target_pairs={{0,4},{1,5},{2,6},{3,7},{4,8},{5,9},{6,10},{7,11},{8,12},{9,13},{1... | collective-permute-start | bytes 1572872 | tf_op jit(solution)/shard_map/ppermute | solution.py:31
  471.9 13.6 %collective-permute-start.22 = (f32[2,4096,16]{1,2,0:T(8,128)S(1)}, f32[2,4096,16]{1,2,0:T(8,128)S(1)}, u32[]{:S(2)}, u32[]{:S(2)}) collective-permute-start(f32[2,4096,16]{1,2,0:T(8,128)S(1)} %add.221), channel_id=1, source_target_pairs={{0,16},{1,17},{2,18},{3,19},{4,20},{5,21},{6,22},{7,23},{8,24},{9,... | collective-permute-start | bytes 1572872 | tf_op jit(solution)/shard_map/ppermute | solution.py:31
  485.5 10.6 %collective-permute-done.22 = f32[2,4096,16]{1,2,0:T(8,128)S(1)} collective-permute-done((f32[2,4096,16]{1,2,0:T(8,128)S(1)}, f32[2,4096,16]{1,2,0:T(8,128)S(1)}, u32[]{:S(2)}, u32[]{:S(2)}) %collective-permute-start.22) | collective-permute-done | bytes 524320 | tf_op jit(solution)/shard_map/ppermute | solution.py:31
  496.2 9.2 %collective-permute-start.23 = (f32[2,4096,16]{1,2,0:T(8,128)S(1)}, f32[2,4096,16]{1,2,0:T(8,128)S(1)}, u32[]{:S(2)}, u32[]{:S(2)}) collective-permute-start(f32[2,4096,16]{1,2,0:T(8,128)S(1)} %add.222), channel_id=1, source_target_pairs={{0,32},{1,33},{2,34},{3,35},{4,36},{5,37},{6,38},{7,39},{8,40},{9,... | collective-permute-start | bytes 1572872 | tf_op jit(solution)/shard_map/ppermute | solution.py:31
  (74 shorter events, 168.0 us)
Async XLA Ops:
  38.6 14.7 %collective-permute-start = (f32[2,4096,16]{1,2,0:T(8,128)S(1)}, f32[2,4096,16]{1,2,0:T(8,128)S(1)}, u32[]{:S(2)}, u32[]{:S(2)}) collective-permute-start(f32[2,4096,16]{1,2,0:T(8,128)S(1)} %slice_bitcast_fusion.3), channel_id=1, source_target_pairs={{0,1},{1,2},{2,3},{3,4},{4,5},{5,6},{6,7},{7,8},{8,9},{9,10},{10,1... | collective-permute-start | bytes 1572872 | tf_op jit(solution)/shard_map/ppermute | solution.py:31
  53.3 16.5 %collective-permute-start.1 = (f32[2,4096,16]{1,2,0:T(8,128)S(1)}, f32[2,4096,16]{1,2,0:T(8,128)S(1)}, u32[]{:S(2)}, u32[]{:S(2)}) collective-permute-start(f32[2,4096,16]{1,2,0:T(8,128)S(1)} %fusion.76), channel_id=1, source_target_pairs={{0,2},{1,3},{2,4},{3,5},{4,6},{5,7},{6,8},{7,9},{8,10},{9,11},{10,... | collective-permute-start | bytes 1572872 | tf_op jit(solution)/shard_map/ppermute | solution.py:31
  69.9 16.4 %collective-permute-start.2 = (f32[2,4096,16]{1,2,0:T(8,128)S(1)}, f32[2,4096,16]{1,2,0:T(8,128)S(1)}, u32[]{:S(2)}, u32[]{:S(2)}) collective-permute-start(f32[2,4096,16]{1,2,0:T(8,128)S(1)} %add.183), channel_id=1, source_target_pairs={{0,4},{1,5},{2,6},{3,7},{4,8},{5,9},{6,10},{7,11},{8,12},{9,13},{1... | collective-permute-start | bytes 1572872 | tf_op jit(solution)/shard_map/ppermute | solution.py:31
  86.4 14.1 %collective-permute-start.3 = (f32[2,4096,16]{1,2,0:T(8,128)S(1)}, f32[2,4096,16]{1,2,0:T(8,128)S(1)}, u32[]{:S(2)}, u32[]{:S(2)}) collective-permute-start(f32[2,4096,16]{1,2,0:T(8,128)S(1)} %add.184), channel_id=1, source_target_pairs={{0,8},{1,9},{2,10},{3,11},{4,12},{5,13},{6,14},{7,15},{8,16},{9,17... | collective-permute-start | bytes 1572872 | tf_op jit(solution)/shard_map/ppermute | solution.py:31
  100.6 18.2 %collective-permute-start.4 = (f32[2,4096,16]{1,2,0:T(8,128)S(1)}, f32[2,4096,16]{1,2,0:T(8,128)S(1)}, u32[]{:S(2)}, u32[]{:S(2)}) collective-permute-start(f32[2,4096,16]{1,2,0:T(8,128)S(1)} %add.185), channel_id=1, source_target_pairs={{0,16},{1,17},{2,18},{3,19},{4,20},{5,21},{6,22},{7,23},{8,24},{9,... | collective-permute-start | bytes 1572872 | tf_op jit(solution)/shard_map/ppermute | solution.py:31
  118.9 18.7 %collective-permute-start.5 = (f32[2,4096,16]{1,2,0:T(8,128)S(1)}, f32[2,4096,16]{1,2,0:T(8,128)S(1)}, u32[]{:S(2)}, u32[]{:S(2)}) collective-permute-start(f32[2,4096,16]{1,2,0:T(8,128)S(1)} %add.186), channel_id=1, source_target_pairs={{0,32},{1,33},{2,34},{3,35},{4,36},{5,37},{6,38},{7,39},{8,40},{9,... | collective-permute-start | bytes 1572872 | tf_op jit(solution)/shard_map/ppermute | solution.py:31
  174.9 8.9 %collective-permute-start.6 = (f32[2,4096,16]{1,2,0:T(8,128)S(1)}, f32[2,4096,16]{1,2,0:T(8,128)S(1)}, u32[]{:S(2)}, u32[]{:S(2)}) collective-permute-start(f32[2,4096,16]{1,2,0:T(8,128)S(1)} %slice_bitcast_fusion.2), channel_id=1, source_target_pairs={{0,1},{1,2},{2,3},{3,4},{4,5},{5,6},{6,7},{7,8},{8,9},{9,10},{10,1... | collective-permute-start | bytes 1572872 | tf_op jit(solution)/shard_map/ppermute | solution.py:31
  183.9 12.5 %collective-permute-start.7 = (f32[2,4096,16]{1,2,0:T(8,128)S(1)}, f32[2,4096,16]{1,2,0:T(8,128)S(1)}, u32[]{:S(2)}, u32[]{:S(2)}) collective-permute-start(f32[2,4096,16]{1,2,0:T(8,128)S(1)} %fusion.77), channel_id=1, source_target_pairs={{0,2},{1,3},{2,4},{3,5},{4,6},{5,7},{6,8},{7,9},{8,10},{9,11},{10,... | collective-permute-start | bytes 1572872 | tf_op jit(solution)/shard_map/ppermute | solution.py:31
  196.5 14.8 %collective-permute-start.8 = (f32[2,4096,16]{1,2,0:T(8,128)S(1)}, f32[2,4096,16]{1,2,0:T(8,128)S(1)}, u32[]{:S(2)}, u32[]{:S(2)}) collective-permute-start(f32[2,4096,16]{1,2,0:T(8,128)S(1)} %add.195), channel_id=1, source_target_pairs={{0,4},{1,5},{2,6},{3,7},{4,8},{5,9},{6,10},{7,11},{8,12},{9,13},{1... | collective-permute-start | bytes 1572872 | tf_op jit(solution)/shard_map/ppermute | solution.py:31
  211.4 17.7 %collective-permute-start.9 = (f32[2,4096,16]{1,2,0:T(8,128)S(1)}, f32[2,4096,16]{1,2,0:T(8,128)S(1)}, u32[]{:S(2)}, u32[]{:S(2)}) collective-permute-start(f32[2,4096,16]{1,2,0:T(8,128)S(1)} %add.196), channel_id=1, source_target_pairs={{0,8},{1,9},{2,10},{3,11},{4,12},{5,13},{6,14},{7,15},{8,16},{9,17... | collective-permute-start | bytes 1572872 | tf_op jit(solution)/shard_map/ppermute | solution.py:31
  229.1 22.6 %collective-permute-start.10 = (f32[2,4096,16]{1,2,0:T(8,128)S(1)}, f32[2,4096,16]{1,2,0:T(8,128)S(1)}, u32[]{:S(2)}, u32[]{:S(2)}) collective-permute-start(f32[2,4096,16]{1,2,0:T(8,128)S(1)} %add.197), channel_id=1, source_target_pairs={{0,16},{1,17},{2,18},{3,19},{4,20},{5,21},{6,22},{7,23},{8,24},{9,... | collective-permute-start | bytes 1572872 | tf_op jit(solution)/shard_map/ppermute | solution.py:31
  251.8 13.5 %collective-permute-start.11 = (f32[2,4096,16]{1,2,0:T(8,128)S(1)}, f32[2,4096,16]{1,2,0:T(8,128)S(1)}, u32[]{:S(2)}, u32[]{:S(2)}) collective-permute-start(f32[2,4096,16]{1,2,0:T(8,128)S(1)} %add.198), channel_id=1, source_target_pairs={{0,32},{1,33},{2,34},{3,35},{4,36},{5,37},{6,38},{7,39},{8,40},{9,... | collective-permute-start | bytes 1572872 | tf_op jit(solution)/shard_map/ppermute | solution.py:31
  300.4 8.0 %collective-permute-start.12 = (f32[2,4096,16]{1,2,0:T(8,128)S(1)}, f32[2,4096,16]{1,2,0:T(8,128)S(1)}, u32[]{:S(2)}, u32[]{:S(2)}) collective-permute-start(f32[2,4096,16]{1,2,0:T(8,128)S(1)} %slice_bitcast_fusion.1), channel_id=1, source_target_pairs={{0,1},{1,2},{2,3},{3,4},{4,5},{5,6},{6,7},{7,8},{8,9},{9,10},{10,1... | collective-permute-start | bytes 1572872 | tf_op jit(solution)/shard_map/ppermute | solution.py:31
  308.4 10.4 %collective-permute-start.13 = (f32[2,4096,16]{1,2,0:T(8,128)S(1)}, f32[2,4096,16]{1,2,0:T(8,128)S(1)}, u32[]{:S(2)}, u32[]{:S(2)}) collective-permute-start(f32[2,4096,16]{1,2,0:T(8,128)S(1)} %fusion.78), channel_id=1, source_target_pairs={{0,2},{1,3},{2,4},{3,5},{4,6},{5,7},{6,8},{7,9},{8,10},{9,11},{10,... | collective-permute-start | bytes 1572872 | tf_op jit(solution)/shard_map/ppermute | solution.py:31
  318.9 18.6 %collective-permute-start.14 = (f32[2,4096,16]{1,2,0:T(8,128)S(1)}, f32[2,4096,16]{1,2,0:T(8,128)S(1)}, u32[]{:S(2)}, u32[]{:S(2)}) collective-permute-start(f32[2,4096,16]{1,2,0:T(8,128)S(1)} %add.207), channel_id=1, source_target_pairs={{0,4},{1,5},{2,6},{3,7},{4,8},{5,9},{6,10},{7,11},{8,12},{9,13},{1... | collective-permute-start | bytes 1572872 | tf_op jit(solution)/shard_map/ppermute | solution.py:31
  337.5 12.7 %collective-permute-start.15 = (f32[2,4096,16]{1,2,0:T(8,128)S(1)}, f32[2,4096,16]{1,2,0:T(8,128)S(1)}, u32[]{:S(2)}, u32[]{:S(2)}) collective-permute-start(f32[2,4096,16]{1,2,0:T(8,128)S(1)} %add.208), channel_id=1, source_target_pairs={{0,8},{1,9},{2,10},{3,11},{4,12},{5,13},{6,14},{7,15},{8,16},{9,17... | collective-permute-start | bytes 1572872 | tf_op jit(solution)/shard_map/ppermute | solution.py:31
  350.2 21.9 %collective-permute-start.16 = (f32[2,4096,16]{1,2,0:T(8,128)S(1)}, f32[2,4096,16]{1,2,0:T(8,128)S(1)}, u32[]{:S(2)}, u32[]{:S(2)}) collective-permute-start(f32[2,4096,16]{1,2,0:T(8,128)S(1)} %add.209), channel_id=1, source_target_pairs={{0,16},{1,17},{2,18},{3,19},{4,20},{5,21},{6,22},{7,23},{8,24},{9,... | collective-permute-start | bytes 1572872 | tf_op jit(solution)/shard_map/ppermute | solution.py:31
  372.1 14.9 %collective-permute-start.17 = (f32[2,4096,16]{1,2,0:T(8,128)S(1)}, f32[2,4096,16]{1,2,0:T(8,128)S(1)}, u32[]{:S(2)}, u32[]{:S(2)}) collective-permute-start(f32[2,4096,16]{1,2,0:T(8,128)S(1)} %add.210), channel_id=1, source_target_pairs={{0,32},{1,33},{2,34},{3,35},{4,36},{5,37},{6,38},{7,39},{8,40},{9,... | collective-permute-start | bytes 1572872 | tf_op jit(solution)/shard_map/ppermute | solution.py:31
  424.3 8.0 %collective-permute-start.18 = (f32[2,4096,16]{1,2,0:T(8,128)S(1)}, f32[2,4096,16]{1,2,0:T(8,128)S(1)}, u32[]{:S(2)}, u32[]{:S(2)}) collective-permute-start(f32[2,4096,16]{1,2,0:T(8,128)S(1)} %slice_bitcast_fusion), channel_id=1, source_target_pairs={{0,1},{1,2},{2,3},{3,4},{4,5},{5,6},{6,7},{7,8},{8,9},{9,10},{10,1... | collective-permute-start | bytes 1572872 | tf_op jit(solution)/shard_map/ppermute | solution.py:31
  432.4 8.0 %collective-permute-start.19 = (f32[2,4096,16]{1,2,0:T(8,128)S(1)}, f32[2,4096,16]{1,2,0:T(8,128)S(1)}, u32[]{:S(2)}, u32[]{:S(2)}) collective-permute-start(f32[2,4096,16]{1,2,0:T(8,128)S(1)} %fusion.79), channel_id=1, source_target_pairs={{0,2},{1,3},{2,4},{3,5},{4,6},{5,7},{6,8},{7,9},{8,10},{9,11},{10,... | collective-permute-start | bytes 1572872 | tf_op jit(solution)/shard_map/ppermute | solution.py:31
  440.4 20.0 %collective-permute-start.20 = (f32[2,4096,16]{1,2,0:T(8,128)S(1)}, f32[2,4096,16]{1,2,0:T(8,128)S(1)}, u32[]{:S(2)}, u32[]{:S(2)}) collective-permute-start(f32[2,4096,16]{1,2,0:T(8,128)S(1)} %add.219), channel_id=1, source_target_pairs={{0,4},{1,5},{2,6},{3,7},{4,8},{5,9},{6,10},{7,11},{8,12},{9,13},{1... | collective-permute-start | bytes 1572872 | tf_op jit(solution)/shard_map/ppermute | solution.py:31
  460.4 11.4 %collective-permute-start.21 = (f32[2,4096,16]{1,2,0:T(8,128)S(1)}, f32[2,4096,16]{1,2,0:T(8,128)S(1)}, u32[]{:S(2)}, u32[]{:S(2)}) collective-permute-start(f32[2,4096,16]{1,2,0:T(8,128)S(1)} %add.220), channel_id=1, source_target_pairs={{0,8},{1,9},{2,10},{3,11},{4,12},{5,13},{6,14},{7,15},{8,16},{9,17... | collective-permute-start | bytes 1572872 | tf_op jit(solution)/shard_map/ppermute | solution.py:31
  471.9 24.2 %collective-permute-start.22 = (f32[2,4096,16]{1,2,0:T(8,128)S(1)}, f32[2,4096,16]{1,2,0:T(8,128)S(1)}, u32[]{:S(2)}, u32[]{:S(2)}) collective-permute-start(f32[2,4096,16]{1,2,0:T(8,128)S(1)} %add.221), channel_id=1, source_target_pairs={{0,16},{1,17},{2,18},{3,19},{4,20},{5,21},{6,22},{7,23},{8,24},{9,... | collective-permute-start | bytes 1572872 | tf_op jit(solution)/shard_map/ppermute | solution.py:31
  496.2 15.8 %collective-permute-start.23 = (f32[2,4096,16]{1,2,0:T(8,128)S(1)}, f32[2,4096,16]{1,2,0:T(8,128)S(1)}, u32[]{:S(2)}, u32[]{:S(2)}) collective-permute-start(f32[2,4096,16]{1,2,0:T(8,128)S(1)} %add.222), channel_id=1, source_target_pairs={{0,32},{1,33},{2,34},{3,35},{4,36},{5,37},{6,38},{7,39},{8,40},{9,... | collective-permute-start | bytes 1572872 | tf_op jit(solution)/shard_map/ppermute | solution.py:31
  (5 other events, 80.3 us)
where the time goes:
time: 521 us; the launch traced here: 514 us
  waiting for transfers between devices  184 us (35%)
  starting transfers between devices  178 us (34%)
  matrix products  134 us (26%)
  other arithmetic  16.1 us (3%)
    ppermute x24, waiting for transfers between devices, local_run(): inclusive = inclusive + lax.ppermute(inclusive, 'time', pairs)  184 us
    ppermute x24, starting transfers between devices, local_run(): inclusive = inclusive + lax.ppermute(inclusive, 'time', pairs)  178 us
    dot_general x4, matrix products, drift_of(): jnp.einsum('kbnh,hc->kbnc', act.astype(jnp.bfloat16), w_out, preferred_el...  134 us
    another operation x4, other arithmetic, local_run(): running = jnp.cumsum(drift, axis=0)  10.8 us
  transfers between devices with their start and end apart: 24, of which 24 were waited for; matrix products, arithmetic and copies ran while one was open for 0% of the time, Pallas kernels for 0%

commit v1 on v0

v1 whole, which is shorter than its diff:
```python
import functools

import jax
import jax.numpy as jnp
from jax import lax
from jax.experimental import pallas as pl
from jax.experimental.pallas import tpu as pltpu
from jax.sharding import PartitionSpec as P

SWEEPS = 4
LIN = 2.0 * 0.7978845608028654
CUB = 8.0 * 0.7978845608028654 * 0.044715
LANES = 128
F32 = jnp.float32
BF16 = jnp.bfloat16


def kernel(n_time, x_hbm, w_in_ref, w_out_ref, scale_ref, shift_ref, step_ref, out_ref,
           x_own, w_in32, mods, steps, step_own, w3, w_all, rhs0, rhs_all, raw_all, stage, run_sum,
           pre0, pre1, act0, act1,
           local_sem, mod_send, mod_recv, step_send, step_recv, out_send, out_recv):
    hidden = w_in_ref.shape[1]
    chunks = hidden // 128
    tiles = x_hbm.shape[2] // LANES
    me = lax.axis_index("time")
    samp = me // tiles
    off = pl.multiple_of(lax.rem(me, tiles) * LANES, LANES)
    pres, acts = (pre0, pre1), (act0, act1)

    copies = [
        pltpu.make_async_copy(x_hbm.at[samp, :, pl.ds(off, LANES)], x_own, local_sem.at[0]),
        pltpu.make_async_copy(scale_ref, mods.at[me, 0], local_sem.at[1]),
        pltpu.make_async_copy(shift_ref, mods.at[me, 1], local_sem.at[2]),
    ]
    for c in copies:
        c.start()
    for a in range(2):
        step_own[a:a + 1, :] = jnp.full((1, LANES), step_ref[a], F32)
    w_in32[...] = w_in_ref[...].astype(F32)
    for c in copies:
        c.wait()

    def mod_copy(slot, peer):
        return pltpu.make_async_remote_copy(
            src_ref=mods.at[slot], dst_ref=mods.at[slot], send_sem=mod_send, recv_sem=mod_recv.at[slot],
            device_id={"time": peer}, device_id_type=pl.DeviceIdType.MESH)

    def step_copy(peer):
        return pltpu.make_async_remote_copy(
            src_ref=step_own, dst_ref=steps.at[me], send_sem=step_send, recv_sem=step_recv,
            device_id={"time": peer}, device_id_type=pl.DeviceIdType.MESH)

    def out_copy(pair):
        return pltpu.make_async_remote_copy(
            src_ref=stage.at[pair], dst_ref=out_ref.at[:, samp, :, pl.ds(off, LANES)],
            send_sem=out_send, recv_sem=out_recv,
            device_id={"time": pair}, device_id_type=pl.DeviceIdType.MESH)

    def send_out(pair):
        @pl.when(pair != me)
        def _():
            out_copy(pair).start()

    own_step = pltpu.make_async_copy(step_own, steps.at[me], local_sem.at[0])
    own_step.start()

    @pl.loop(1, n_time)
    def _(r):
        mod_copy(me, lax.rem(me + n_time - r, n_time)).start()

    @pl.loop(1, n_time)
    def _(r):
        step_copy(lax.rem(me + n_time - r, n_time)).start()

    x_bf = x_own[...].astype(BF16)
    one_row = jnp.where(lax.broadcasted_iota(jnp.int32, (16, LANES), 0) == 0, 1.0, 0.0).astype(BF16)
    zero_blk = jnp.zeros((64, LANES), BF16)

    def fill_const(ref):
        for a in range(2):
            ref[64 * a:64 * a + 64, LANES * (1 - a):LANES * (2 - a)] = zero_blk
            ref[64 * a + 48:64 * a + 64, LANES * a:LANES * (a + 1)] = one_row

    def fill_x(ref, a, val):
        for m in range(3):
            ref[64 * a + 16 * m:64 * a + 16 * m + 16, LANES * a:LANES * (a + 1)] = val

    fill_const(rhs0)
    for a in range(2):
        fill_x(rhs0, a, x_bf)

    first_row = lax.broadcasted_iota(jnp.int32, (16, hidden), 0) == 0

    def prep(pair):
        for a in range(2):
            s = 0.5 * (1.0 + mods[pair, 0, a:a + 1, :].astype(F32))
            b = 0.5 * mods[pair, 1, a:a + 1, :].astype(F32)
            p = w_in32[...] * s
            for m in range(3):
                q = p.astype(BF16)
                w3[64 * a + 16 * m:64 * a + 16 * m + 16, :] = q
                if m < 2:
                    p = p - q.astype(F32)
            w3[64 * a + 48:64 * a + 64, :] = jnp.where(first_row, b, 0.0).astype(BF16)
        for c in range(chunks):
            w_all[pair, 128 * c:128 * c + 128, :] = w3[:, 128 * c:128 * c + 128].T

    def body(a_pair, b_on, c_on, par, rhs=None):
        pre_w, pre_r, act_w, act_r = pres[par], pres[1 - par], acts[1 - par], acts[par]
        total = None
        if a_pair is not None and rhs is None:
            rhs = rhs_all.at[a_pair]
        for c in range(chunks):
            rows = slice(128 * c, 128 * c + 128)
            if c_on and c % 2 == 0:
                k_rows = slice(128 * c, min(128 * c + 256, hidden))
                part = jnp.dot(w_out_ref[:, k_rows], act_r[k_rows, :], preferred_element_type=F32)
                total = part if total is None else total + part
            if a_pair is not None:
                pre_w[rows, :] = jnp.dot(w_all[a_pair, rows, :], rhs[...], preferred_element_type=F32)
            if b_on:
                for k in range(8):
                    sub = slice(128 * c + 16 * k, 128 * c + 16 * k + 16)
                    h = pre_r[sub, :]
                    t = jnp.tanh(h * (LIN + CUB * (h * h)))
                    act_w[sub, :] = (h + h * t).astype(BF16)
        return total

    def drift_to_x(pair, raw, emit):
        total = jnp.where(pair == 0, 0.0, run_sum[...])
        for a in range(2):
            emit(a, x_own[...] + total)
            total = total + raw[:, LANES * a:LANES * (a + 1)] * steps[pair, a:a + 1, :]
        run_sum[...] = total

    def emit_rhs(pair):
        def emit(a, val):
            fill_x(rhs_all.at[pair], a, val.astype(BF16))
        return emit

    def emit_stage(pair):
        def emit(a, val):
            stage[pair, a] = val
        return emit

    def rot(i):
        return lax.rem(me + i, n_time)

    prep(me)
    mod_copy(rot(1), me).wait_recv()
    prep(rot(1))
    body(rot(0), False, False, 0, rhs0)

    def first(t, par):
        mod_copy(rot(t + 1), me).wait_recv()
        prep(rot(t + 1))
        fill_const(rhs_all.at[t])
        raw = body(rot(t), True, True, par, rhs0)
        raw_all[rot(t - 2)] = raw

    mod_copy(rot(2), me).wait_recv()
    prep(rot(2))
    fill_const(rhs_all.at[0])
    fill_const(rhs_all.at[1])
    body(rot(1), True, False, 1, rhs0)

    @pl.loop(0, (n_time - 4) // 2)
    def _(i):
        first(2 * i + 2, 0)
        first(2 * i + 3, 1)

    first(n_time - 2, 0)
    fill_const(rhs_all.at[n_time - 1])
    raw_all[rot(n_time - 3)] = body(rot(n_time - 1), True, True, 1, rhs0)
    raw_all[rot(n_time - 2)] = body(None, True, True, 0)
    raw_all[rot(n_time - 1)] = body(None, False, True, 1)

    others = pl.ds(0, n_time - 1)
    own_step.wait()
    pltpu.make_async_copy(steps.at[others], steps.at[others], step_recv).wait()

    def spread(pair):
        drift_to_x(pair, raw_all[pair], emit_rhs(pair))

    def mid(t, par, first_sweep):
        c_pair = lax.rem(t - 2, n_time)
        raw = body(lax.rem(t, n_time), True, True, par)
        return c_pair, raw

    @pl.loop(0, n_time // 4)
    def _(i):
        for k in range(4):
            spread(4 * i + k)

    body(0, False, False, 0)
    body(1, True, False, 1)

    @pl.loop(0, (SWEEPS - 2) * n_time // 2)
    def _(i):
        for par in range(2):
            c_pair, raw = mid(2 * i + 2 + par, par, False)
            drift_to_x(c_pair, raw, emit_rhs(c_pair))

    @pl.loop(0, (n_time - 2) // 2)
    def _(i):
        for par in range(2):
            pair = 2 * i + par
            if par == 0:
                @pl.when(i > 0)
                def _():
                    send_out(pair - 1)
            else:
                send_out(pair - 1)
            raw = body(pair + 2, True, True, par)
            drift_to_x(pair, raw, emit_stage(pair))

    send_out(n_time - 3)
    drift_to_x(n_time - 2, body(None, True, True, 0), emit_stage(n_time - 2))
    send_out(n_time - 2)
    drift_to_x(n_time - 1, body(None, False, True, 1), emit_stage(n_time - 1))
    send_out(n_time - 1)

    own_out = pltpu.make_async_copy(stage.at[me], out_ref.at[:, samp, :, pl.ds(off, LANES)], local_sem.at[0])
    own_out.start()
    own_out.wait()
    for ref, sem in ((stage, out_send), (mods, mod_send), (steps, step_send), (stage, out_recv)):
        pltpu.make_async_copy(ref.at[others], ref.at[others], sem).wait()


def solution(mesh):
    n_time = mesh.shape["time"]

    def local_run(x_init, w_in, w_out, mod_scale, mod_shift, step_size):
        x_t = jnp.transpose(x_init, (0, 2, 1))
        chan, hidden = w_in.shape
        batch, tokens = x_init.shape[0], x_init.shape[1]
        vmem = pl.BlockSpec(memory_space=pltpu.VMEM)
        out = pl.pallas_call(
            functools.partial(kernel, n_time),
            out_shape=jax.ShapeDtypeStruct((2, batch, chan, tokens), F32),
            in_specs=[pl.BlockSpec(memory_space=pl.ANY), vmem, vmem, vmem, vmem,
                      pl.BlockSpec(memory_space=pltpu.SMEM)],
            out_specs=vmem,
            scratch_shapes=[
                pltpu.VMEM((chan, LANES), F32),
                pltpu.VMEM((chan, hidden), F32),
                pltpu.VMEM((n_time, 2, 2, hidden), BF16),
                pltpu.VMEM((n_time, 2, LANES), F32),
                pltpu.VMEM((2, LANES), F32),
                pltpu.VMEM((128, hidden), BF16),
                pltpu.VMEM((n_time, hidden, 128), BF16),
                pltpu.VMEM((128, 2 * LANES), BF16),
                pltpu.VMEM((n_time, 128, 2 * LANES), BF16),
                pltpu.VMEM((n_time, chan, 2 * LANES), F32),
                pltpu.VMEM((n_time, 2, chan, LANES), F32),
                pltpu.VMEM((chan, LANES), F32),
                pltpu.VMEM((hidden, 2 * LANES), F32),
                pltpu.VMEM((hidden, 2 * LANES), F32),
                pltpu.VMEM((hidden, 2 * LANES), BF16),
                pltpu.VMEM((hidden, 2 * LANES), BF16),
                pltpu.SemaphoreType.DMA((3,)),
                pltpu.SemaphoreType.DMA,
                pltpu.SemaphoreType.DMA((n_time,)),
                pltpu.SemaphoreType.DMA,
                pltpu.SemaphoreType.DMA,
                pltpu.SemaphoreType.DMA,
                pltpu.SemaphoreType.DMA,
            ],
            compiler_params=pltpu.CompilerParams(has_side_effects=True, vmem_limit_bytes=58 * 1024 * 1024),
            name="picard",
        )(x_t, w_in, w_out.T, mod_scale, mod_shift, step_size)
        return jnp.transpose(out, (0, 1, 3, 2))

    return jax.shard_map(
        local_run,
        mesh=mesh,
        in_specs=(P(("part", "data"), None, None), P(None, None), P(None, None), P("time", None), P("time", None), P("time")),
        out_specs=P("time", ("part", "data"), None, None),
        check_vma=False,
    )
```

time: 521 us -> 161 us (0.31)
  waiting for transfers between devices: 184 us -> 0 us
  starting transfers between devices: 178 us -> 0 us
  Pallas kernels: 0 us -> 156 us
  matrix products: 134 us -> 0 us
  other arithmetic: 16.1 us -> 0 us
    ppermute x24 -> x0, waiting for transfers between devices: 184 us -> none  [local_run(): inclusive = inclusive + lax.ppermute(inclusive, 'time', pairs)]
    ppermute x24 -> x0, starting transfers between devices: 178 us -> none  [local_run(): inclusive = inclusive + lax.ppermute(inclusive, 'time', pairs)]
    pallas_call x0 -> x1, Pallas kernels: none -> 156 us  [local_run(): pl.pallas_call(functools.partial(kernel, n_time), out_shape=jax.ShapeDtyp...]
    dot_general x4 -> x0, matrix products: 134 us -> none  [drift_of(): jnp.einsum('kbnh,hc->kbnc', act.astype(jnp.bfloat16), w_out, preferred_el...]
    another operation x4 -> x0, other arithmetic: 10.8 us -> none  [local_run(): running = jnp.cumsum(drift, axis=0)]
  transfers between devices with their start and end apart: 24 -> 0, of which waited for: 24 -> 0; matrix products, arithmetic and copies ran while one was open for 0% -> 0% of each run, Pallas kernels for 0% -> 0%
where the time goes in v1:
time: 161 us; the launch traced here: 159 us
  Pallas kernels  156 us (97%)
  local copies, waits for them, and re-layouts  2.27 us (1%)
    pallas_call x1, Pallas kernels, local_run(): pl.pallas_call(functools.partial(kernel, n_time), out_shape=jax.ShapeDtyp...  156 us

profile of v1, /device:TPU:0, one launch (start us, length us, event | category | flops | bytes accessed | tf_op | source)
XLA Modules:
  0.0 158.5 jit_solution(11606261164027317927)
XLA Ops:
  0.0 156.2 %picard.1 = f32[2,2,16,4096]{3,2,1,0:T(8,128)} custom-call(f32[2,16,4096]{2,1,0:T(8,128)} %bitcast.4, bf16[16,1152]{1,0:T(8,128)(2,1)} %w_in_ref.1, bf16[16,1152]{1,0:T(8,128)(2,1)} %bitcast.5, bf16[2,1152]{1,0:T(2,128)(2,1)} %scale_ref.1, bf16[2,1152]{1,0:T(2,128)(2,1)} %shift_ref.1, f32[2]{0:T(128)} %step_ref.1), custom_call_target="tpu_custom_call" | custom-call | tf_op jit(solution)/shard_map/picard/pallas_call | solution.py:238
  156.2 2.3 %copy.8 = f32[2,2,4096,16]{2,3,1,0:T(8,128)} copy(f32[2,2,4096,16]{2,3,1,0:T(8,128)} %bitcast.3) | data formatting | bytes 2097152

commit v2 on v1

--- a/solution.py
+++ b/solution.py
@@ -16,8 +16,8 @@
 
 
 def kernel(n_time, x_hbm, w_in_ref, w_out_ref, scale_ref, shift_ref, step_ref, out_ref,
-           x_own, w_in32, mods, steps, step_own, w3, w_all, rhs0, rhs_all, raw_all, stage, run_sum,
-           pre0, pre1, act0, act1,
+           x_own, w_in32, mods, steps, step_own, w_all, rhs0, rhs_all, raw_all, stage, run_sum,
+           pre0, pre1, act0, act1, wp0, wp1,
            local_sem, mod_send, mod_recv, step_send, step_recv, out_send, out_recv):
     hidden = w_in_ref.shape[1]
     chunks = hidden // 128
@@ -25,7 +25,7 @@
     me = lax.axis_index("time")
     samp = me // tiles
     off = pl.multiple_of(lax.rem(me, tiles) * LANES, LANES)
-    pres, acts = (pre0, pre1), (act0, act1)
+    pres, acts, wps = (pre0, pre1), (act0, act1), (wp0, wp1)
 
     copies = [
         pltpu.make_async_copy(x_hbm.at[samp, :, pl.ds(off, LANES)], x_own, local_sem.at[0]),
@@ -89,27 +89,31 @@
     for a in range(2):
         fill_x(rhs0, a, x_bf)
 
-    first_row = lax.broadcasted_iota(jnp.int32, (16, hidden), 0) == 0
-
-    def prep(pair):
+    first_row = lax.broadcasted_iota(jnp.int32, (16, 128), 0) == 0
+
+    def prep(pair, c, w_ref):
+        cols = slice(128 * c, 128 * c + 128)
+        blocks = []
         for a in range(2):
-            s = 0.5 * (1.0 + mods[pair, 0, a:a + 1, :].astype(F32))
-            b = 0.5 * mods[pair, 1, a:a + 1, :].astype(F32)
-            p = w_in32[...] * s
+            s = 0.5 * (1.0 + mods[pair, 0, a:a + 1, cols].astype(F32))
+            b = 0.5 * mods[pair, 1, a:a + 1, cols].astype(F32)
+            p = w_in32[:, cols] * s
             for m in range(3):
                 q = p.astype(BF16)
-                w3[64 * a + 16 * m:64 * a + 16 * m + 16, :] = q
+                blocks.append(q)
                 if m < 2:
                     p = p - q.astype(F32)
-            w3[64 * a + 48:64 * a + 64, :] = jnp.where(first_row, b, 0.0).astype(BF16)
-        for c in range(chunks):
-            w_all[pair, 128 * c:128 * c + 128, :] = w3[:, 128 * c:128 * c + 128].T
-
-    def body(a_pair, b_on, c_on, par, rhs=None):
+            blocks.append(jnp.where(first_row, b, 0.0).astype(BF16))
+        w_t = jnp.concatenate(blocks, axis=0).T
+        w_ref[cols, :] = w_t
+        w_all[pair, cols, :] = w_t
+
+    def body(a_pair, b_on, c_on, par, rhs=None, nxt=None):
         pre_w, pre_r, act_w, act_r = pres[par], pres[1 - par], acts[1 - par], acts[par]
         total = None
-        if a_pair is not None and rhs is None:
-            rhs = rhs_all.at[a_pair]
+        if a_pair is not None:
+            w = w_all.at[a_pair] if rhs is None else wps[par]
+            rhs = rhs_all.at[a_pair] if rhs is None else rhs
         for c in range(chunks):
             rows = slice(128 * c, 128 * c + 128)
             if c_on and c % 2 == 0:
@@ -117,7 +121,9 @@
                 part = jnp.dot(w_out_ref[:, k_rows], act_r[k_rows, :], preferred_element_type=F32)
                 total = part if total is None else total + part
             if a_pair is not None:
-                pre_w[rows, :] = jnp.dot(w_all[a_pair, rows, :], rhs[...], preferred_element_type=F32)
+                pre_w[rows, :] = jnp.dot(w[rows, :], rhs[...], preferred_element_type=F32)
+            if nxt is not None:
+                prep(nxt, c, wps[1 - par])
             if b_on:
                 for k in range(8):
                     sub = slice(128 * c + 16 * k, 128 * c + 16 * k + 16)
@@ -146,32 +152,31 @@
     def rot(i):
         return lax.rem(me + i, n_time)
 
-    prep(me)
+    for c in range(chunks):
+        prep(me, c, wps[0])
     mod_copy(rot(1), me).wait_recv()
-    prep(rot(1))
-    body(rot(0), False, False, 0, rhs0)
-
-    def first(t, par):
-        mod_copy(rot(t + 1), me).wait_recv()
-        prep(rot(t + 1))
-        fill_const(rhs_all.at[t])
-        raw = body(rot(t), True, True, par, rhs0)
-        raw_all[rot(t - 2)] = raw
-
+    body(rot(0), False, False, 0, rhs0, rot(1))
     mod_copy(rot(2), me).wait_recv()
-    prep(rot(2))
+    body(rot(1), True, False, 1, rhs0, rot(2))
     fill_const(rhs_all.at[0])
     fill_const(rhs_all.at[1])
-    body(rot(1), True, False, 1, rhs0)
+
+    def first(t, par):
+        raw_all[rot(t - 2)] = body(rot(t), True, True, par, rhs0, rot(t + 1))
+        fill_const(rhs_all.at[t])
 
     @pl.loop(0, (n_time - 4) // 2)
     def _(i):
-        first(2 * i + 2, 0)
-        first(2 * i + 3, 1)
-
+        t = 2 * i + 2
+        mod_copy(rot(t + 1), me).wait_recv()
+        mod_copy(rot(t + 2), me).wait_recv()
+        first(t, 0)
+        first(t + 1, 1)
+
+    mod_copy(rot(n_time - 1), me).wait_recv()
     first(n_time - 2, 0)
+    raw_all[rot(n_time - 3)] = body(rot(n_time - 1), True, True, 1, rhs0)
     fill_const(rhs_all.at[n_time - 1])
-    raw_all[rot(n_time - 3)] = body(rot(n_time - 1), True, True, 1, rhs0)
     raw_all[rot(n_time - 2)] = body(None, True, True, 0)
     raw_all[rot(n_time - 1)] = body(None, False, True, 1)
 
@@ -182,11 +187,6 @@
     def spread(pair):
         drift_to_x(pair, raw_all[pair], emit_rhs(pair))
 
-    def mid(t, par, first_sweep):
-        c_pair = lax.rem(t - 2, n_time)
-        raw = body(lax.rem(t, n_time), True, True, par)
-        return c_pair, raw
-
     @pl.loop(0, n_time // 4)
     def _(i):
         for k in range(4):
@@ -197,9 +197,11 @@
 
     @pl.loop(0, (SWEEPS - 2) * n_time // 2)
     def _(i):
+        t = 2 * i + 2
+        raws = [body(lax.rem(t + par, n_time), True, True, par) for par in range(2)]
         for par in range(2):
-            c_pair, raw = mid(2 * i + 2 + par, par, False)
-            drift_to_x(c_pair, raw, emit_rhs(c_pair))
+            pair = lax.rem(2 * i + par, n_time)
+            drift_to_x(pair, raws[par], emit_rhs(pair))
 
     @pl.loop(0, (n_time - 2) // 2)
     def _(i):
@@ -247,7 +249,6 @@
                 pltpu.VMEM((n_time, 2, 2, hidden), BF16),
                 pltpu.VMEM((n_time, 2, LANES), F32),
                 pltpu.VMEM((2, LANES), F32),
-                pltpu.VMEM((128, hidden), BF16),
                 pltpu.VMEM((n_time, hidden, 128), BF16),
                 pltpu.VMEM((128, 2 * LANES), BF16),
                 pltpu.VMEM((n_time, 128, 2 * LANES), BF16),
@@ -258,6 +259,8 @@
                 pltpu.VMEM((hidden, 2 * LANES), F32),
                 pltpu.VMEM((hidden, 2 * LANES), BF16),
                 pltpu.VMEM((hidden, 2 * LANES), BF16),
+                pltpu.VMEM((hidden, 128), BF16),
+                pltpu.VMEM((hidden, 128), BF16),
                 pltpu.SemaphoreType.DMA((3,)),
                 pltpu.SemaphoreType.DMA,
                 pltpu.SemaphoreType.DMA((n_time,)),

time: 161 us -> 140 us (0.87)
  Pallas kernels: 156 us -> 135 us
    pallas_call x1, Pallas kernels: 156 us -> 135 us  [local_run(): pl.pallas_call(functools.partial(kernel, n_time), out_shape=jax.ShapeDtyp...]
where the time goes in v2:
time: 140 us; the launch traced here: 138 us
  Pallas kernels  135 us (96%)
  local copies, waits for them, and re-layouts  2.27 us (2%)
    pallas_call x1, Pallas kernels, local_run(): pl.pallas_call(functools.partial(kernel, n_time), out_shape=jax.ShapeDtyp...  135 us

profile of v2, /device:TPU:0, one launch (start us, length us, event | category | flops | bytes accessed | tf_op | source)
XLA Modules:
  0.0 137.7 jit_solution(3786869859459261095)
XLA Ops:
  0.0 135.4 %picard.1 = f32[2,2,16,4096]{3,2,1,0:T(8,128)} custom-call(f32[2,16,4096]{2,1,0:T(8,128)} %bitcast.4, bf16[16,1152]{1,0:T(8,128)(2,1)} %w_in_ref.1, bf16[16,1152]{1,0:T(8,128)(2,1)} %bitcast.5, bf16[2,1152]{1,0:T(2,128)(2,1)} %scale_ref.1, bf16[2,1152]{1,0:T(2,128)(2,1)} %shift_ref.1, f32[2]{0:T(128)} %step_ref.1), custom_call_target="tpu_custom_call" | custom-call | tf_op jit(solution)/shard_map/picard/pallas_call | solution.py:240
  135.4 2.3 %copy.8 = f32[2,2,4096,16]{2,3,1,0:T(8,128)} copy(f32[2,2,4096,16]{2,3,1,0:T(8,128)} %bitcast.3) | data formatting | bytes 2097152

commit v3 on v2

--- a/solution.py
+++ b/solution.py
@@ -8,6 +8,7 @@
 from jax.sharding import PartitionSpec as P
 
 SWEEPS = 4
+AHEAD = 16
 LIN = 2.0 * 0.7978845608028654
 CUB = 8.0 * 0.7978845608028654 * 0.044715
 LANES = 128
@@ -15,10 +16,10 @@
 BF16 = jnp.bfloat16
 
 
-def kernel(n_time, x_hbm, w_in_ref, w_out_ref, scale_ref, shift_ref, step_ref, out_ref,
-           x_own, w_in32, mods, steps, step_own, w_all, rhs0, rhs_all, raw_all, stage, run_sum,
+def kernel(n_time, x_hbm, w_in_ref, w_out_ref, scale_ref, shift_ref, step_ref, out_ref, fix_ref,
+           x_own, w_in32, mods, steps, step_own, w_all, rhs0, rhs_all, raw_all, stage, fix, run_sum,
            pre0, pre1, act0, act1, wp0, wp1,
-           local_sem, mod_send, mod_recv, step_send, step_recv, out_send, out_recv):
+           local_sem, mod_send, mod_recv, step_send, step_recv, out_send, out_recv, fix_send, fix_recv):
     hidden = w_in_ref.shape[1]
     chunks = hidden // 128
     tiles = x_hbm.shape[2] // LANES
@@ -50,27 +51,30 @@
             src_ref=step_own, dst_ref=steps.at[me], send_sem=step_send, recv_sem=step_recv,
             device_id={"time": peer}, device_id_type=pl.DeviceIdType.MESH)
 
-    def out_copy(pair):
-        return pltpu.make_async_remote_copy(
-            src_ref=stage.at[pair], dst_ref=out_ref.at[:, samp, :, pl.ds(off, LANES)],
-            send_sem=out_send, recv_sem=out_recv,
-            device_id={"time": pair}, device_id_type=pl.DeviceIdType.MESH)
-
-    def send_out(pair):
+    def send_to(pair, src, dst, send, recv):
         @pl.when(pair != me)
         def _():
-            out_copy(pair).start()
+            pltpu.make_async_remote_copy(
+                src_ref=src.at[pair], dst_ref=dst.at[:, samp, :, pl.ds(off, LANES)], send_sem=send, recv_sem=recv,
+                device_id={"time": pair}, device_id_type=pl.DeviceIdType.MESH).start()
+
+    def send_base(pair):
+        send_to(pair, stage, out_ref, out_send, out_recv)
+
+    def send_fix(pair):
+        send_to(pair, fix, fix_ref, fix_send, fix_recv)
 
     own_step = pltpu.make_async_copy(step_own, steps.at[me], local_sem.at[0])
     own_step.start()
 
-    @pl.loop(1, n_time)
+    def send_mods(r):
+        peer = lax.rem(me + n_time - r, n_time)
+        mod_copy(me, peer).start()
+        step_copy(peer).start()
+
+    @pl.loop(1, AHEAD + 1)
     def _(r):
-        mod_copy(me, lax.rem(me + n_time - r, n_time)).start()
-
-    @pl.loop(1, n_time)
-    def _(r):
-        step_copy(lax.rem(me + n_time - r, n_time)).start()
+        send_mods(r)
 
     x_bf = x_own[...].astype(BF16)
     one_row = jnp.where(lax.broadcasted_iota(jnp.int32, (16, LANES), 0) == 0, 1.0, 0.0).astype(BF16)
@@ -141,12 +145,13 @@
 
     def emit_rhs(pair):
         def emit(a, val):
+            stage[pair, a] = val
             fill_x(rhs_all.at[pair], a, val.astype(BF16))
         return emit
 
-    def emit_stage(pair):
+    def emit_fix(pair):
         def emit(a, val):
-            stage[pair, a] = val
+            fix[pair, a] = (val - stage[pair, a]).astype(BF16)
         return emit
 
     def rot(i):
@@ -167,11 +172,14 @@
 
     @pl.loop(0, (n_time - 4) // 2)
     def _(i):
-        t = 2 * i + 2
-        mod_copy(rot(t + 1), me).wait_recv()
-        mod_copy(rot(t + 2), me).wait_recv()
-        first(t, 0)
-        first(t + 1, 1)
+        for par in range(2):
+            t = 2 * i + 2 + par
+
+            @pl.when(t - 1 + AHEAD < n_time)
+            def _():
+                send_mods(t - 1 + AHEAD)
+            mod_copy(rot(t + 1), me).wait_recv()
+            first(t, par)
 
     mod_copy(rot(n_time - 1), me).wait_recv()
     first(n_time - 2, 0)
@@ -197,36 +205,48 @@
 
     @pl.loop(0, (SWEEPS - 2) * n_time // 2)
     def _(i):
-        t = 2 * i + 2
-        raws = [body(lax.rem(t + par, n_time), True, True, par) for par in range(2)]
         for par in range(2):
-            pair = lax.rem(2 * i + par, n_time)
-            drift_to_x(pair, raws[par], emit_rhs(pair))
+            step = 2 * i + par
+            pair = lax.rem(step, n_time)
+
+            @pl.when(step >= (SWEEPS - 3) * n_time + 2)
+            def _():
+                send_base(pair - 2)
+            raw = body(lax.rem(step + 2, n_time), True, True, par)
+            drift_to_x(pair, raw, emit_rhs(pair))
 
     @pl.loop(0, (n_time - 2) // 2)
     def _(i):
         for par in range(2):
             pair = 2 * i + par
-            if par == 0:
-                @pl.when(i > 0)
-                def _():
-                    send_out(pair - 1)
-            else:
-                send_out(pair - 1)
+
+            @pl.when(i > 0)
+            def _():
+                send_fix(pair - 2)
+
+            @pl.when(i == 0)
+            def _():
+                send_base(n_time - 2 + par)
             raw = body(pair + 2, True, True, par)
-            drift_to_x(pair, raw, emit_stage(pair))
-
-    send_out(n_time - 3)
-    drift_to_x(n_time - 2, body(None, True, True, 0), emit_stage(n_time - 2))
-    send_out(n_time - 2)
-    drift_to_x(n_time - 1, body(None, False, True, 1), emit_stage(n_time - 1))
-    send_out(n_time - 1)
-
-    own_out = pltpu.make_async_copy(stage.at[me], out_ref.at[:, samp, :, pl.ds(off, LANES)], local_sem.at[0])
-    own_out.start()
-    own_out.wait()
-    for ref, sem in ((stage, out_send), (mods, mod_send), (steps, step_send), (stage, out_recv)):
+            drift_to_x(pair, raw, emit_fix(pair))
+
+    send_fix(n_time - 4)
+    send_fix(n_time - 3)
+    drift_to_x(n_time - 2, body(None, True, True, 0), emit_fix(n_time - 2))
+    send_fix(n_time - 2)
+    drift_to_x(n_time - 1, body(None, False, True, 1), emit_fix(n_time - 1))
+    send_fix(n_time - 1)
+
+    own = [
+        pltpu.make_async_copy(stage.at[me], out_ref.at[:, samp, :, pl.ds(off, LANES)], local_sem.at[0]),
+        pltpu.make_async_copy(fix.at[me], fix_ref.at[:, samp, :, pl.ds(off, LANES)], local_sem.at[1]),
+    ]
+    for c in own:
+        c.start()
+    for ref, sem in ((mods, mod_send), (steps, step_send), (stage, out_send), (fix, fix_send), (stage, out_recv), (fix, fix_recv)):
         pltpu.make_async_copy(ref.at[others], ref.at[others], sem).wait()
+    for c in own:
+        c.wait()
 
 
 def solution(mesh):
@@ -237,12 +257,12 @@
         chan, hidden = w_in.shape
         batch, tokens = x_init.shape[0], x_init.shape[1]
         vmem = pl.BlockSpec(memory_space=pltpu.VMEM)
-        out = pl.pallas_call(
+        base, fix = pl.pallas_call(
             functools.partial(kernel, n_time),
-            out_shape=jax.ShapeDtypeStruct((2, batch, chan, tokens), F32),
+            out_shape=[jax.ShapeDtypeStruct((2, batch, chan, tokens), t) for t in (F32, BF16)],
             in_specs=[pl.BlockSpec(memory_space=pl.ANY), vmem, vmem, vmem, vmem,
                       pl.BlockSpec(memory_space=pltpu.SMEM)],
-            out_specs=vmem,
+            out_specs=[vmem, vmem],
             scratch_shapes=[
                 pltpu.VMEM((chan, LANES), F32),
                 pltpu.VMEM((chan, hidden), F32),
@@ -254,6 +274,7 @@
                 pltpu.VMEM((n_time, 128, 2 * LANES), BF16),
                 pltpu.VMEM((n_time, chan, 2 * LANES), F32),
                 pltpu.VMEM((n_time, 2, chan, LANES), F32),
+                pltpu.VMEM((n_time, 2, chan, LANES), BF16),
                 pltpu.VMEM((chan, LANES), F32),
                 pltpu.VMEM((hidden, 2 * LANES), F32),
                 pltpu.VMEM((hidden, 2 * LANES), F32),
@@ -268,11 +289,13 @@
                 pltpu.SemaphoreType.DMA,
                 pltpu.SemaphoreType.DMA,
                 pltpu.SemaphoreType.DMA,
+                pltpu.SemaphoreType.DMA,
+                pltpu.SemaphoreType.DMA,
             ],
             compiler_params=pltpu.CompilerParams(has_side_effects=True, vmem_limit_bytes=58 * 1024 * 1024),
             name="picard",
         )(x_t, w_in, w_out.T, mod_scale, mod_shift, step_size)
-        return jnp.transpose(out, (0, 1, 3, 2))
+        return jnp.transpose(base + fix.astype(F32), (0, 1, 3, 2))
 
     return jax.shard_map(
         local_run,

time: 140 us -> 134 us (0.957); the launches traced: 138 us -> 133 us
  Pallas kernels: 135 us -> 131 us
  other arithmetic: 0 us -> 2.42 us
  local copies, waits for them, and re-layouts: 2.27 us -> 0 us
    pallas_call x1, Pallas kernels: 135 us -> 131 us  [local_run(): pl.pallas_call(functools.partial(kernel, n_time), out_shape=[jax.ShapeDty...]
    transpose x0 -> x1, other arithmetic: none -> 2.42 us  [local_run(): return jnp.transpose(base + fix.astype(F32), (0, 1, 3, 2))]
    unnamed x1 -> x0, local copies, waits for them, and re-layouts: 2.27 us -> none
where the time goes in v3:
time: 134 us; the launch traced here: 133 us
  Pallas kernels  131 us (98%)
  other arithmetic  2.42 us (2%)
    pallas_call x1, Pallas kernels, local_run(): pl.pallas_call(functools.partial(kernel, n_time), out_shape=[jax.ShapeDty...  131 us

profile of v3, /device:TPU:0, one launch (start us, length us, event | category | flops | bytes accessed | tf_op | source)
XLA Modules:
  0.0 133.3 jit_solution(9141220629640687494)
XLA Ops:
  0.0 130.9 %picard.1 = (f32[2,2,16,4096]{3,2,1,0:T(8,128)}, bf16[2,2,16,4096]{3,2,1,0:T(8,128)(2,1)}) custom-call(f32[2,16,4096]{2,1,0:T(8,128)} %bitcast.4, bf16[16,1152]{1,0:T(8,128)(2,1)} %w_in_ref.1, bf16[16,1152]{1,0:T(8,128)(2,1)} %bitcast.5, bf16[2,1152]{1,0:T(2,128)(2,1)} %scale_ref.1, bf16[2,1152]{1,0:T(2,128)(2,1)} %shift_ref.1, f32[2]{0:T(128)} %step_ref.1), custom_call_target="tpu_custom_call" | custom-call | tf_op jit(solution)/shard_map/picard/pallas_call | solution.py:260
  130.9 2.4 %add_bitcast_fusion = f32[2,2,4096,16]{2,3,1,0:T(8,128)} fusion(f32[2,2,16,4096]{3,2,1,0:T(8,128)} %get-tuple-element.7, bf16[2,2,16,4096]{3,2,1,0:T(8,128)(2,1)} %get-tuple-element.8), kind=kLoop, calls=%fused_computation | loop fusion | flops 524288 | bytes 2621440 | tf_op jit(solution)/shard_map/transpose | solution.py:298

commit v4 on v3

--- a/solution.py
+++ b/solution.py
@@ -8,7 +8,7 @@
 from jax.sharding import PartitionSpec as P
 
 SWEEPS = 4
-AHEAD = 16
+UNROLL = 8
 LIN = 2.0 * 0.7978845608028654
 CUB = 8.0 * 0.7978845608028654 * 0.044715
 LANES = 128
@@ -17,7 +17,7 @@
 
 
 def kernel(n_time, x_hbm, w_in_ref, w_out_ref, scale_ref, shift_ref, step_ref, out_ref, fix_ref,
-           x_own, w_in32, mods, steps, step_own, w_all, rhs0, rhs_all, raw_all, stage, fix, run_sum,
+           x_own, w_in32, mods, steps, step_own, w_all, rhs0, rhs_all, raw_all, raw_blk, stage, fix, run_sum,
            pre0, pre1, act0, act1, wp0, wp1,
            local_sem, mod_send, mod_recv, step_send, step_recv, out_send, out_recv, fix_send, fix_recv):
     hidden = w_in_ref.shape[1]
@@ -72,7 +72,7 @@
         mod_copy(me, peer).start()
         step_copy(peer).start()
 
-    @pl.loop(1, AHEAD + 1)
+    @pl.loop(1, 3 * UNROLL + 1)
     def _(r):
         send_mods(r)
 
@@ -93,15 +93,14 @@
     for a in range(2):
         fill_x(rhs0, a, x_bf)
 
-    first_row = lax.broadcasted_iota(jnp.int32, (16, 128), 0) == 0
-
-    def prep(pair, c, w_ref):
-        cols = slice(128 * c, 128 * c + 128)
+    first_row = lax.broadcasted_iota(jnp.int32, (16, hidden), 0) == 0
+
+    def prep(pair, w_ref):
         blocks = []
         for a in range(2):
-            s = 0.5 * (1.0 + mods[pair, 0, a:a + 1, cols].astype(F32))
-            b = 0.5 * mods[pair, 1, a:a + 1, cols].astype(F32)
-            p = w_in32[:, cols] * s
+            s = 0.5 * (1.0 + mods[pair, 0, a:a + 1, :].astype(F32))
+            b = 0.5 * mods[pair, 1, a:a + 1, :].astype(F32)
+            p = w_in32[...] * s
             for m in range(3):
                 q = p.astype(BF16)
                 blocks.append(q)
@@ -109,8 +108,8 @@
                     p = p - q.astype(F32)
             blocks.append(jnp.where(first_row, b, 0.0).astype(BF16))
         w_t = jnp.concatenate(blocks, axis=0).T
-        w_ref[cols, :] = w_t
-        w_all[pair, cols, :] = w_t
+        w_ref[...] = w_t
+        w_all[pair] = w_t
 
     def body(a_pair, b_on, c_on, par, rhs=None, nxt=None):
         pre_w, pre_r, act_w, act_r = pres[par], pres[1 - par], acts[1 - par], acts[par]
@@ -118,22 +117,18 @@
         if a_pair is not None:
             w = w_all.at[a_pair] if rhs is None else wps[par]
             rhs = rhs_all.at[a_pair] if rhs is None else rhs
-        for c in range(chunks):
-            rows = slice(128 * c, 128 * c + 128)
-            if c_on and c % 2 == 0:
-                k_rows = slice(128 * c, min(128 * c + 256, hidden))
-                part = jnp.dot(w_out_ref[:, k_rows], act_r[k_rows, :], preferred_element_type=F32)
-                total = part if total is None else total + part
-            if a_pair is not None:
-                pre_w[rows, :] = jnp.dot(w[rows, :], rhs[...], preferred_element_type=F32)
-            if nxt is not None:
-                prep(nxt, c, wps[1 - par])
-            if b_on:
-                for k in range(8):
-                    sub = slice(128 * c + 16 * k, 128 * c + 16 * k + 16)
-                    h = pre_r[sub, :]
-                    t = jnp.tanh(h * (LIN + CUB * (h * h)))
-                    act_w[sub, :] = (h + h * t).astype(BF16)
+        if a_pair is not None:
+            pre_w[...] = jnp.dot(w[...], rhs[...], preferred_element_type=F32)
+        if c_on:
+            total = jnp.dot(w_out_ref[...], act_r[...], preferred_element_type=F32)
+        if nxt is not None:
+            prep(nxt, wps[1 - par])
+        if b_on:
+            for c in range(chunks):
+                rows = slice(128 * c, 128 * c + 128)
+                h = pre_r[rows, :]
+                t = jnp.tanh(h * (LIN + CUB * (h * h)))
+                act_w[rows, :] = (h + h * t).astype(BF16)
         return total
 
     def drift_to_x(pair, raw, emit):
@@ -157,34 +152,44 @@
     def rot(i):
         return lax.rem(me + i, n_time)
 
-    for c in range(chunks):
-        prep(me, c, wps[0])
-    mod_copy(rot(1), me).wait_recv()
-    body(rot(0), False, False, 0, rhs0, rot(1))
-    mod_copy(rot(2), me).wait_recv()
-    body(rot(1), True, False, 1, rhs0, rot(2))
-    fill_const(rhs_all.at[0])
-    fill_const(rhs_all.at[1])
-
-    def first(t, par):
-        raw_all[rot(t - 2)] = body(rot(t), True, True, par, rhs0, rot(t + 1))
+    def wait_mods(lo, count):
+        for k in range(count):
+            mod_copy(rot(lo + k), me).wait_recv()
+
+    def block(lo, hi, f):
+        @pl.loop(lo // 2, hi // 2, unroll=True)
+        def _(kk):
+            for par in range(2):
+                f(2 * kk + par, par)
+
+    def first(t, par, b_on=True, c_on=True, nxt=True):
+        raw = body(rot(t), b_on, c_on, par, rhs0, rot(t + 1) if nxt else None)
+        if c_on:
+            raw_all[rot(t - 2)] = raw
         fill_const(rhs_all.at[t])
 
-    @pl.loop(0, (n_time - 4) // 2)
+    prep(me, wps[0])
+    wait_mods(1, 2)
+    first(0, 0, False, False)
+    first(1, 1, True, False)
+    wait_mods(3, UNROLL - 2)
+    block(2, UNROLL, first)
+
+    @pl.loop(1, n_time // UNROLL - 1)
     def _(i):
-        for par in range(2):
-            t = 2 * i + 2 + par
-
-            @pl.when(t - 1 + AHEAD < n_time)
+        for k in range(UNROLL):
+            r = UNROLL * (i + 2) + 1 + k
+
+            @pl.when(r < n_time)
             def _():
-                send_mods(t - 1 + AHEAD)
-            mod_copy(rot(t + 1), me).wait_recv()
-            first(t, par)
-
-    mod_copy(rot(n_time - 1), me).wait_recv()
+                send_mods(r)
+        wait_mods(UNROLL * i + 1, UNROLL)
+        block(0, UNROLL, lambda k, par: first(UNROLL * i + k, par))
+
+    wait_mods(n_time - UNROLL + 1, UNROLL - 1)
+    block(n_time - UNROLL, n_time - 2, first)
     first(n_time - 2, 0)
-    raw_all[rot(n_time - 3)] = body(rot(n_time - 1), True, True, 1, rhs0)
-    fill_const(rhs_all.at[n_time - 1])
+    first(n_time - 1, 1, nxt=False)
     raw_all[rot(n_time - 2)] = body(None, True, True, 0)
     raw_all[rot(n_time - 1)] = body(None, False, True, 1)
 
@@ -192,46 +197,70 @@
     own_step.wait()
     pltpu.make_async_copy(steps.at[others], steps.at[others], step_recv).wait()
 
-    def spread(pair):
-        drift_to_x(pair, raw_all[pair], emit_rhs(pair))
-
-    @pl.loop(0, n_time // 4)
+    @pl.loop(0, n_time // 2 - 1)
     def _(i):
-        for k in range(4):
-            spread(4 * i + k)
-
-    body(0, False, False, 0)
-    body(1, True, False, 1)
-
-    @pl.loop(0, (SWEEPS - 2) * n_time // 2)
+        for k in range(2):
+            drift_to_x(2 * i + k, raw_all[2 * i + k], emit_rhs(2 * i + k))
+
+    def finish_block(i):
+        @pl.loop(0, UNROLL, unroll=True)
+        def _(k):
+            pair = lax.rem(UNROLL * i + k - 2 + n_time, n_time)
+            drift_to_x(pair, raw_blk[k], emit_rhs(pair))
+
+    per = n_time // UNROLL
+    base_from = (SWEEPS - 3) * n_time
+
+    def mid(k, par, t=None):
+        raw_blk[k] = body(k if t is None else t, True, True, par)
+
+    for k in range(2):
+        raw_blk[k] = raw_all[n_time - 2 + k]
+        body(k, k >= 1, False, k)
+    block(2, UNROLL, mid)
+
+    @pl.loop(1, (SWEEPS - 2) * per)
     def _(i):
-        for par in range(2):
-            step = 2 * i + par
-            pair = lax.rem(step, n_time)
-
-            @pl.when(step >= (SWEEPS - 3) * n_time + 2)
+        for k in range(UNROLL):
+            step = UNROLL * (i - 2) + k - 2
+
+            @pl.when(step >= base_from)
             def _():
-                send_base(pair - 2)
-            raw = body(lax.rem(step + 2, n_time), True, True, par)
-            drift_to_x(pair, raw, emit_rhs(pair))
-
-    @pl.loop(0, (n_time - 2) // 2)
+                send_base(step - base_from)
+        finish_block(i - 1)
+        block(0, UNROLL, lambda k, par: mid(k, par, lax.rem(UNROLL * i + k, n_time)))
+
+    @pl.loop(0, UNROLL)
+    def _(k):
+        send_base(n_time - 2 * UNROLL - 2 + k)
+    finish_block((SWEEPS - 2) * per - 1)
+    for k in range(2):
+        drift_to_x(n_time - 2 + k, body(k, True, True, k), emit_rhs(n_time - 2 + k))
+
+    def late(t, par):
+        drift_to_x(t - 2, body(t, True, True, par), emit_fix(t - 2))
+
+    block(2, UNROLL, late)
+
+    @pl.loop(0, UNROLL + 2)
+    def _(k):
+        send_base(n_time - UNROLL - 2 + k)
+
+    @pl.loop(0, UNROLL - 2)
+    def _(k):
+        send_fix(k)
+
+    @pl.loop(1, per)
     def _(i):
-        for par in range(2):
-            pair = 2 * i + par
-
-            @pl.when(i > 0)
+        for k in range(UNROLL):
+            @pl.when(i > 1)
             def _():
-                send_fix(pair - 2)
-
-            @pl.when(i == 0)
-            def _():
-                send_base(n_time - 2 + par)
-            raw = body(pair + 2, True, True, par)
-            drift_to_x(pair, raw, emit_fix(pair))
-
-    send_fix(n_time - 4)
-    send_fix(n_time - 3)
+                send_fix(UNROLL * (i - 1) + k - 2)
+        block(0, UNROLL, lambda k, par: late(UNROLL * i + k, par))
+
+    @pl.loop(0, UNROLL)
+    def _(k):
+        send_fix(n_time - UNROLL - 2 + k)
     drift_to_x(n_time - 2, body(None, True, True, 0), emit_fix(n_time - 2))
     send_fix(n_time - 2)
     drift_to_x(n_time - 1, body(None, False, True, 1), emit_fix(n_time - 1))
@@ -273,6 +302,7 @@
                 pltpu.VMEM((128, 2 * LANES), BF16),
                 pltpu.VMEM((n_time, 128, 2 * LANES), BF16),
                 pltpu.VMEM((n_time, chan, 2 * LANES), F32),
+                pltpu.VMEM((UNROLL, chan, 2 * LANES), F32),
                 pltpu.VMEM((n_time, 2, chan, LANES), F32),
                 pltpu.VMEM((n_time, 2, chan, LANES), BF16),
                 pltpu.VMEM((chan, LANES), F32),

time: 134 us -> 123 us (0.918)
  Pallas kernels: 131 us -> 120 us
    pallas_call x1, Pallas kernels: 131 us -> 120 us  [local_run(): pl.pallas_call(functools.partial(kernel, n_time), out_shape=[jax.ShapeDty...]
where the time goes in v4:
time: 123 us; the launch traced here: 122 us
  Pallas kernels  120 us (98%)
  other arithmetic  2.42 us (2%)
    pallas_call x1, Pallas kernels, local_run(): pl.pallas_call(functools.partial(kernel, n_time), out_shape=[jax.ShapeDty...  120 us

profile of v4, /device:TPU:0, one launch (start us, length us, event | category | flops | bytes accessed | tf_op | source)
XLA Modules:
  0.0 122.3 jit_solution(5785429338170031794)
XLA Ops:
  0.0 119.9 %picard.1 = (f32[2,2,16,4096]{3,2,1,0:T(8,128)}, bf16[2,2,16,4096]{3,2,1,0:T(8,128)(2,1)}) custom-call(f32[2,16,4096]{2,1,0:T(8,128)} %bitcast.4, bf16[16,1152]{1,0:T(8,128)(2,1)} %w_in_ref.1, bf16[16,1152]{1,0:T(8,128)(2,1)} %bitcast.5, bf16[2,1152]{1,0:T(2,128)(2,1)} %scale_ref.1, bf16[2,1152]{1,0:T(2,128)(2,1)} %shift_ref.1, f32[2]{0:T(128)} %step_ref.1), custom_call_target="tpu_custom_call" | custom-call | tf_op jit(solution)/shard_map/picard/pallas_call | solution.py:289
  119.9 2.4 %add_bitcast_fusion = f32[2,2,4096,16]{2,3,1,0:T(8,128)} fusion(f32[2,2,16,4096]{3,2,1,0:T(8,128)} %get-tuple-element.7, bf16[2,2,16,4096]{3,2,1,0:T(8,128)(2,1)} %get-tuple-element.8), kind=kLoop, calls=%fused_computation | loop fusion | flops 524288 | bytes 2621440 | tf_op jit(solution)/shard_map/transpose | solution.py:328

commit v5 on v4

--- a/solution.py
+++ b/solution.py
@@ -9,8 +9,9 @@
 
 SWEEPS = 4
 UNROLL = 8
-LIN = 2.0 * 0.7978845608028654
-CUB = 8.0 * 0.7978845608028654 * 0.044715
+ROOT = 0.7978845608028654
+CUBE = (ROOT * 0.044715) ** (1.0 / 3.0)
+LIN = ROOT / CUBE
 LANES = 128
 F32 = jnp.float32
 BF16 = jnp.bfloat16
@@ -18,7 +19,7 @@
 
 def kernel(n_time, x_hbm, w_in_ref, w_out_ref, scale_ref, shift_ref, step_ref, out_ref, fix_ref,
            x_own, w_in32, mods, steps, step_own, w_all, rhs0, rhs_all, raw_all, raw_blk, stage, fix, run_sum,
-           pre0, pre1, act0, act1, wp0, wp1,
+           pre0, pre1, act0, act1, wp0, wp1, w_out3,
            local_sem, mod_send, mod_recv, step_send, step_recv, out_send, out_recv, fix_send, fix_recv):
     hidden = w_in_ref.shape[1]
     chunks = hidden // 128
@@ -77,7 +78,7 @@
         send_mods(r)
 
     x_bf = x_own[...].astype(BF16)
-    one_row = jnp.where(lax.broadcasted_iota(jnp.int32, (16, LANES), 0) == 0, 1.0, 0.0).astype(BF16)
+    one_row = jnp.where(lax.broadcasted_iota(jnp.int32, (16, LANES), 0) < 3, 1.0, 0.0).astype(BF16)
     zero_blk = jnp.zeros((64, LANES), BF16)
 
     def fill_const(ref):
@@ -93,20 +94,27 @@
     for a in range(2):
         fill_x(rhs0, a, x_bf)
 
-    first_row = lax.broadcasted_iota(jnp.int32, (16, hidden), 0) == 0
+    row_of = lax.broadcasted_iota(jnp.int32, (8, hidden), 0)
+
+    def terms(p):
+        out = []
+        for m in range(3):
+            out.append(p.astype(BF16))
+            if m < 2:
+                p = p - out[m].astype(F32)
+        return out
+
+    w_out3[...] = jnp.concatenate(terms(w_out_ref[...].astype(F32) * (0.5 / CUBE)), axis=0)
 
     def prep(pair, w_ref):
         blocks = []
         for a in range(2):
-            s = 0.5 * (1.0 + mods[pair, 0, a:a + 1, :].astype(F32))
-            b = 0.5 * mods[pair, 1, a:a + 1, :].astype(F32)
-            p = w_in32[...] * s
-            for m in range(3):
-                q = p.astype(BF16)
-                blocks.append(q)
-                if m < 2:
-                    p = p - q.astype(F32)
-            blocks.append(jnp.where(first_row, b, 0.0).astype(BF16))
+            blocks += terms(w_in32[...] * (CUBE * (1.0 + mods[pair, 0, a:a + 1, :].astype(F32))))
+            b = CUBE * mods[pair, 1, a:a + 1, :].astype(F32)
+            rows = jnp.zeros((8, hidden), F32)
+            for m, q in enumerate(terms(b)):
+                rows = jnp.where(row_of == m, q.astype(F32), rows)
+            blocks.append(jnp.concatenate([rows, jnp.zeros((8, hidden), F32)], axis=0).astype(BF16))
         w_t = jnp.concatenate(blocks, axis=0).T
         w_ref[...] = w_t
         w_all[pair] = w_t
@@ -120,14 +128,15 @@
         if a_pair is not None:
             pre_w[...] = jnp.dot(w[...], rhs[...], preferred_element_type=F32)
         if c_on:
-            total = jnp.dot(w_out_ref[...], act_r[...], preferred_element_type=F32)
+            parts = jnp.dot(w_out3[...], act_r[...], preferred_element_type=F32)
+            total = parts[:16] + (parts[16:32] + parts[32:])
         if nxt is not None:
             prep(nxt, wps[1 - par])
         if b_on:
             for c in range(chunks):
                 rows = slice(128 * c, 128 * c + 128)
                 h = pre_r[rows, :]
-                t = jnp.tanh(h * (LIN + CUB * (h * h)))
+                t = jnp.tanh(h * (LIN + h * h))
                 act_w[rows, :] = (h + h * t).astype(BF16)
         return total
 
@@ -250,7 +259,7 @@
     def _(k):
         send_fix(k)
 
-    @pl.loop(1, per)
+    @pl.loop(1, per - 1)
     def _(i):
         for k in range(UNROLL):
             @pl.when(i > 1)
@@ -260,7 +269,15 @@
 
     @pl.loop(0, UNROLL)
     def _(k):
-        send_fix(n_time - UNROLL - 2 + k)
+        send_fix(n_time - 2 * UNROLL - 2 + k)
+
+    @pl.loop(n_time // 2 - UNROLL // 2, n_time // 2)
+    def _(i):
+        for par in range(2):
+            late(2 * i + par, par)
+        for par in range(2):
+            send_fix(2 * i + par - 2)
+
     drift_to_x(n_time - 2, body(None, True, True, 0), emit_fix(n_time - 2))
     send_fix(n_time - 2)
     drift_to_x(n_time - 1, body(None, False, True, 1), emit_fix(n_time - 1))
@@ -312,6 +329,7 @@
                 pltpu.VMEM((hidden, 2 * LANES), BF16),
                 pltpu.VMEM((hidden, 128), BF16),
                 pltpu.VMEM((hidden, 128), BF16),
+                pltpu.VMEM((3 * chan, hidden), BF16),
                 pltpu.SemaphoreType.DMA((3,)),
                 pltpu.SemaphoreType.DMA,
                 pltpu.SemaphoreType.DMA((n_time,)),

time: 123 us -> 118 us (0.959)
  Pallas kernels: 120 us -> 115 us
    pallas_call x1, Pallas kernels: 120 us -> 115 us  [local_run(): pl.pallas_call(functools.partial(kernel, n_time), out_shape=[jax.ShapeDty...]
where the time goes in v5:
time: 118 us
  Pallas kernels  115 us (97%)
  other arithmetic  2.42 us (2%)
    pallas_call x1, Pallas kernels, local_run(): pl.pallas_call(functools.partial(kernel, n_time), out_shape=[jax.ShapeDty...  115 us
    transpose x1, other arithmetic, local_run(): return jnp.transpose(base + fix.astype(F32), (0, 1, 3, 2))  2.42 us

profile of v5, /device:TPU:0, one launch (start us, length us, event | category | flops | bytes accessed | tf_op | source)
XLA Modules:
  0.0 117.8 jit_solution(8562408119947679352)
XLA Ops:
  0.0 115.4 %picard.1 = (f32[2,2,16,4096]{3,2,1,0:T(8,128)}, bf16[2,2,16,4096]{3,2,1,0:T(8,128)(2,1)}) custom-call(f32[2,16,4096]{2,1,0:T(8,128)} %bitcast.4, bf16[16,1152]{1,0:T(8,128)(2,1)} %w_in_ref.1, bf16[16,1152]{1,0:T(8,128)(2,1)} %bitcast.5, bf16[2,1152]{1,0:T(2,128)(2,1)} %scale_ref.1, bf16[2,1152]{1,0:T(2,128)(2,1)} %shift_ref.1, f32[2]{0:T(128)} %step_ref.1), custom_call_target="tpu_custom_call" | custom-call | tf_op jit(solution)/shard_map/picard/pallas_call | solution.py:306
  115.4 2.4 %add_bitcast_fusion = f32[2,2,4096,16]{2,3,1,0:T(8,128)} fusion(f32[2,2,16,4096]{3,2,1,0:T(8,128)} %get-tuple-element.7, bf16[2,2,16,4096]{3,2,1,0:T(8,128)(2,1)} %get-tuple-element.8), kind=kLoop, calls=%fused_computation | loop fusion | flops 524288 | bytes 2621440 | tf_op jit(solution)/shard_map/transpose | solution.py:346

commit v6 on v5

--- a/solution.py
+++ b/solution.py
@@ -28,6 +28,13 @@
     samp = me // tiles
     off = pl.multiple_of(lax.rem(me, tiles) * LANES, LANES)
     pres, acts, wps = (pre0, pre1), (act0, act1), (wp0, wp1)
+
+    barrier = pltpu.get_barrier_semaphore()
+
+    @pl.loop(1, n_time)
+    def _(r):
+        pl.semaphore_signal(
+            barrier, inc=1, device_id={"time": lax.rem(me + r, n_time)}, device_id_type=pl.DeviceIdType.MESH)
 
     copies = [
         pltpu.make_async_copy(x_hbm.at[samp, :, pl.ds(off, LANES)], x_own, local_sem.at[0]),
@@ -69,13 +76,7 @@
     own_step.start()
 
     def send_mods(r):
-        peer = lax.rem(me + n_time - r, n_time)
-        mod_copy(me, peer).start()
-        step_copy(peer).start()
-
-    @pl.loop(1, 3 * UNROLL + 1)
-    def _(r):
-        send_mods(r)
+        mod_copy(me, lax.rem(me + n_time - r, n_time)).start()
 
     x_bf = x_own[...].astype(BF16)
     one_row = jnp.where(lax.broadcasted_iota(jnp.int32, (16, LANES), 0) < 3, 1.0, 0.0).astype(BF16)
@@ -178,12 +179,20 @@
         fill_const(rhs_all.at[t])
 
     prep(me, wps[0])
+    pl.semaphore_wait(barrier, n_time - 1)
+
+    @pl.loop(1, 3 * UNROLL + 1)
+    def _(r):
+        send_mods(r)
+
     wait_mods(1, 2)
     first(0, 0, False, False)
     first(1, 1, True, False)
     wait_mods(3, UNROLL - 2)
     block(2, UNROLL, first)
 
+    spread = -(-(n_time - 1) // (n_time // UNROLL - 2))
+
     @pl.loop(1, n_time // UNROLL - 1)
     def _(i):
         for k in range(UNROLL):
@@ -192,6 +201,14 @@
             @pl.when(r < n_time)
             def _():
                 send_mods(r)
+
+        @pl.loop(0, spread)
+        def _(k):
+            r = (i - 1) * spread + k + 1
+
+            @pl.when(r < n_time)
+            def _():
+                step_copy(lax.rem(me + r, n_time)).start()
         wait_mods(UNROLL * i + 1, UNROLL)
         block(0, UNROLL, lambda k, par: first(UNROLL * i + k, par))
 
@@ -340,7 +357,7 @@
                 pltpu.SemaphoreType.DMA,
                 pltpu.SemaphoreType.DMA,
             ],
-            compiler_params=pltpu.CompilerParams(has_side_effects=True, vmem_limit_bytes=58 * 1024 * 1024),
+            compiler_params=pltpu.CompilerParams(collective_id=0, has_side_effects=True, vmem_limit_bytes=58 * 1024 * 1024),
             name="picard",
         )(x_t, w_in, w_out.T, mod_scale, mod_shift, step_size)
         return jnp.transpose(base + fix.astype(F32), (0, 1, 3, 2))

time: 118 us -> 113 us (0.958)
  Pallas kernels: 115 us -> 110 us
    pallas_call x1, Pallas kernels: 115 us -> 110 us  [local_run(): pl.pallas_call(functools.partial(kernel, n_time), out_shape=[jax.ShapeDty...]
where the time goes in v6:
time: 113 us
  Pallas kernels  110 us (97%)
  other arithmetic  2.42 us (2%)
    pallas_call x1, Pallas kernels, local_run(): pl.pallas_call(functools.partial(kernel, n_time), out_shape=[jax.ShapeDty...  110 us
    transpose x1, other arithmetic, local_run(): return jnp.transpose(base + fix.astype(F32), (0, 1, 3, 2))  2.42 us

profile of v6, /device:TPU:0, one launch (start us, length us, event | category | flops | bytes accessed | tf_op | source)
XLA Modules:
  0.0 112.7 jit_solution(10881307963914506110)
XLA Ops:
  0.0 110.3 %picard.1 = (f32[2,2,16,4096]{3,2,1,0:T(8,128)}, bf16[2,2,16,4096]{3,2,1,0:T(8,128)(2,1)}) custom-call(f32[2,16,4096]{2,1,0:T(8,128)} %bitcast.4, bf16[16,1152]{1,0:T(8,128)(2,1)} %w_in_ref.1, bf16[16,1152]{1,0:T(8,128)(2,1)} %bitcast.5, bf16[2,1152]{1,0:T(2,128)(2,1)} %scale_ref.1, bf16[2,1152]{1,0:T(2,128)(2,1)} %shift_ref.1, f32[2]{0:T(128)} %step_ref.1), custom_call_target="tpu_custom_call" | custom-call | tf_op jit(solution)/shard_map/picard/pallas_call | solution.py:323
  110.3 2.4 %add_bitcast_fusion = f32[2,2,4096,16]{2,3,1,0:T(8,128)} fusion(f32[2,2,16,4096]{3,2,1,0:T(8,128)} %get-tuple-element.7, bf16[2,2,16,4096]{3,2,1,0:T(8,128)(2,1)} %get-tuple-element.8), kind=kLoop, calls=%fused_computation | loop fusion | flops 524288 | bytes 2621440 | tf_op jit(solution)/shard_map/transpose | solution.py:363

commit v7 on v6

--- a/solution.py
+++ b/solution.py
@@ -188,8 +188,12 @@
     wait_mods(1, 2)
     first(0, 0, False, False)
     first(1, 1, True, False)
-    wait_mods(3, UNROLL - 2)
-    block(2, UNROLL, first)
+
+    @pl.loop(1, UNROLL // 2)
+    def _(i):
+        wait_mods(2 * i + 1, 2)
+        for par in range(2):
+            first(2 * i + par, par)
 
     spread = -(-(n_time - 1) // (n_time // UNROLL - 2))
 
@@ -325,7 +329,7 @@
             out_shape=[jax.ShapeDtypeStruct((2, batch, chan, tokens), t) for t in (F32, BF16)],
             in_specs=[pl.BlockSpec(memory_space=pl.ANY), vmem, vmem, vmem, vmem,
                       pl.BlockSpec(memory_space=pltpu.SMEM)],
-            out_specs=[vmem, vmem],
+            out_specs=[pl.BlockSpec(memory_space=pl.ANY)] * 2,
             scratch_shapes=[
                 pltpu.VMEM((chan, LANES), F32),
                 pltpu.VMEM((chan, hidden), F32),

time: 113 us -> 112 us (level)
  no operation moved by 1% of the time
where the time goes in v7:
time: 112 us
  Pallas kernels  109 us (97%)
  other arithmetic  2.42 us (2%)
    pallas_call x1, Pallas kernels, local_run(): pl.pallas_call(functools.partial(kernel, n_time), out_shape=[jax.ShapeDty...  109 us
    transpose x1, other arithmetic, local_run(): return jnp.transpose(base + fix.astype(F32), (0, 1, 3, 2))  2.42 us

profile of v7, /device:TPU:0, one launch (start us, length us, event | category | flops | bytes accessed | tf_op | source)
XLA Modules:
  0.0 111.9 jit_solution(12318302076952796485)
XLA Ops:
  0.0 109.5 %picard.1 = (f32[2,2,16,4096]{3,2,1,0:T(8,128)}, bf16[2,2,16,4096]{3,2,1,0:T(8,128)(2,1)}) custom-call(f32[2,16,4096]{2,1,0:T(8,128)} %bitcast.4, bf16[16,1152]{1,0:T(8,128)(2,1)} %w_in_ref.1, bf16[16,1152]{1,0:T(8,128)(2,1)} %bitcast.5, bf16[2,1152]{1,0:T(2,128)(2,1)} %scale_ref.1, bf16[2,1152]{1,0:T(2,128)(2,1)} %shift_ref.1, f32[2]{0:T(128)} %step_ref.1), custom_call_target="tpu_custom_call" | custom-call | tf_op jit(solution)/shard_map/picard/pallas_call | solution.py:327
  109.5 2.4 %add_bitcast_fusion = f32[2,2,4096,16]{2,3,1,0:T(8,128)} fusion(f32[2,2,16,4096]{3,2,1,0:T(8,128)} %get-tuple-element.7, bf16[2,2,16,4096]{3,2,1,0:T(8,128)(2,1)} %get-tuple-element.8), kind=kLoop, calls=%fused_computation | loop fusion | flops 524288 | bytes 2621440 | tf_op jit(solution)/shard_map/transpose | solution.py:367
